TPU v7x, 32 devices: a whole 2x2x4 slice. The times are simulated.
32 devices in a mesh: row: 8 (over z, x), col: 4 (over y, core).
Axes of the slice: x: 2, y: 2, z: 4, core: 2. Of those that a mesh axis runs over, the one named last changes fastest.
Arguments:
- snapshot: bfloat16 [512, 256, 512], P('row', 'col'), may hold values from -6 to 6
- basis_two: bfloat16 [256, 128], P('col'), may hold values from -0.375 to 0.375
- basis_three: bfloat16 [512, 128], replicated, may hold values from -0.25 to 0.25
Outputs:
- gram: float32 [512, 512], P('row', 'col')
All inputs are finite; a program needn't handle non-finite values.
Results may differ from a plain program's by a relative error of at most 0.0017.
Values may be sent and summed in bfloat16 or wider, within the bound.
No kernel may reach another device: no remote copies, remote signals or barrier semaphores. Data moves between devices by JAX's collectives and lax.ppermute only.
A program may use at most 64 MiB of HBM per device.

v0:
```python
import jax
import jax.numpy as jnp
from jax import lax
from jax.sharding import PartitionSpec as P


def on_device(snapshot, basis_two, basis_three):
    cells_one, cells_two, cells_three = snapshot.shape
    ranks_two = basis_two.shape[1]
    ranks_three = basis_three.shape[1]
    inner = jnp.dot(
        snapshot.reshape(cells_one * cells_two, cells_three),
        basis_three,
        preferred_element_type=jnp.float32,
    )
    inner = inner.astype(jnp.bfloat16).reshape(cells_one, cells_two, ranks_three)
    regrouped = lax.all_to_all(inner, "col", split_axis=2, concat_axis=1, tiled=True)
    whole_factor = lax.all_gather(basis_two, "col", axis=0, tiled=True)
    full = jnp.einsum("abr,bq->qar", regrouped, whole_factor, preferred_element_type=jnp.float32)
    rounded = lax.all_to_all(
        full.astype(jnp.bfloat16), "col", split_axis=0, concat_axis=2, tiled=True
    )
    partial_gram = jnp.einsum(
        "qar,qbr->ab",
        rounded,
        lax.all_gather(rounded, "row", axis=1, tiled=True),
        preferred_element_type=jnp.float32,
    )
    summed_gram = lax.psum_scatter(partial_gram, "col", scatter_dimension=1, tiled=True)
    return summed_gram * (1.0 / (ranks_two * ranks_three))


def solution(mesh):
    in_specs = (P("row", "col", None), P("col", None), P())
    out_specs = P("row", "col")
    return jax.shard_map(
        on_device, mesh=mesh, in_specs=in_specs, out_specs=out_specs, check_vma=False
    )
```

profile of v0, /device:TPU:0, one launch (start us, length us, event | category | flops | bytes accessed | tf_op | source)
XLA Modules:
  0.0 165.3 jit_solution(16451007527104671222)
XLA Ops:
  6.5 0.0 copy-start
  6.5 0.9 copy-done
  7.4 3.4 %convolution_convert_fusion = bf16[4096,128]{1,0:T(8,128)(2,1)S(1)} fusion(bf16[4096,512]{1,0:T(8,128)(2,1)} %bitcast.31, bf16[512,128]{1,0:T(8,128)(2,1)S(1)} %copy-done), kind=kOutput, calls=%fused_computation | convolution fusion | flops 537395200 | bytes 5373952 | tf_op jit(solution)/shard_map/dot_general | solution.py:11
  10.9 0.0 copy-start.1
  10.9 3.0 %copy.20 = bf16[64,64,128]{1,0,2:T(8,128)(2,1)S(1)} copy(bf16[64,64,128]{2,1,0:T(8,128)(2,1)S(1)} %bitcast.32) | data formatting | bytes 2097152 | tf_op jit(solution)/shard_map/reshape | solution.py:16
  13.9 2.6 %reshape.10 = bf16[4,2,65536]{2,1,0:T(2,128)(2,1)} reshape(bf16[128,64,64]{2,1,0:T(8,128)(2,1)S(1)} %bitcast.29) | data formatting | bytes 2097152
  16.5 4.3 %all-to-all-start = ((bf16[4,2,65536]{2,1,0:T(2,128)(2,1)}), bf16[4,2,65536]{2,1,0:T(2,128)(2,1)S(1)}, u32[]{:S(2)}, u32[]{:S(2)}) async-start(bf16[4,2,65536]{2,1,0:T(2,128)(2,1)} %reshape.10), calls=%async_computation | async-start | bytes 2097152 | tf_op jit(solution)/shard_map/all_to_all | solution.py:17
  20.8 0.0 all-gather.2.cloned.1.call-start
  20.8 0.0 copy-done.1
  20.8 15.6 %all_gather.6 = bf16[256,128]{1,0:T(8,128)(2,1)S(1)} all-gather(bf16[64,128]{1,0:T(8,128)(2,1)S(1)} %copy-done.1), channel_id=1, replica_groups=mesh['row'=8,'col'=4] {'col'}, dimensions={0}, use_global_device_ids=true | all-gather | bytes 81920 | tf_op jit(solution)/shard_map/all_gather | solution.py:18
  36.4 0.0 all-to-all-done
  36.4 1.4 reshape.11
  37.8 3.0 %copy.22 = bf16[64,4,64,32]{2,1,3,0:T(4,128)(2,1)} copy(bf16[64,4,64,32]{2,0,3,1:T(8,128)(2,1)S(1)} %bitcast.30) | data formatting | bytes 2097152 | tf_op jit(solution)/shard_map/all_to_all | solution.py:17
  40.8 3.5 %all_to_all.29 = bf16[64,256,32]{1,2,0:T(8,128)(2,1)S(1)} reshape(bf16[64,4,64,32]{2,1,3,0:T(4,128)(2,1)} %copy.22) | data formatting | bytes 2097152 | tf_op jit(solution)/shard_map/all_to_all | solution.py:17
  44.3 0.4 fusion
  44.7 1.7 %copy.23 = bf16[128,64,32]{1,2,0:T(8,128)(2,1)S(1)} copy(bf16[128,64,32]{0,2,1:T(8,128)(2,1)S(1)} %fusion) | data formatting | bytes 1048576 | tf_op jit(solution)/shard_map/convert_element_type | solution.py:21
  46.4 0.9 reshape.12
  47.3 11.2 %all_to_all.36 = bf16[4,2,32768]{2,1,0:T(2,128)(2,1)S(1)} all-to-all(bf16[4,2,32768]{2,1,0:T(2,128)(2,1)S(1)} %reshape.12), channel_id=1, replica_groups=mesh['row'=8,'col'=4] {'col'}, dimensions={0} | all-to-all | bytes 1048576 | tf_op jit(solution)/shard_map/all_to_all | solution.py:20
  58.5 0.7 reshape.13
  59.2 0.1 copy.24
  59.4 1.1 copy.25
  60.5 0.0 all-gather.2.cloned.1.call-update
  60.5 0.0 reduce-scatter.2.cloned.1.call-start
  60.6 73.9 %all-gather.2.cloned.1.call-done = bf16[32,512,128]{2,1,0:T(8,128)(2,1)} async-done(((bf16[32,64,128]{2,1,0:T(8,128)(2,1)}), bf16[32,512,128]{2,1,0:T(8,128)(2,1)}) %all-gather.2.cloned.1.call-update) | async-done | bytes 4194320 | tf_op jit(solution)/shard_map/all_gather | solution.py:26
  134.4 4.2 %convolution_bitcast_fusion = f32[64,512]{1,0:T(8,128)} fusion(bf16[32,64,128]{1,2,0:T(8,128)(2,1)S(1)} %bitcast.28, bf16[32,512,128]{2,1,0:T(8,128)(2,1)} %all-gather.2.cloned.1.call-done), kind=kOutput, calls=%fused_computation.3 | convolution fusion | flops 268435456 | bytes 4849664 | tf_op jit(solution)/shard_map/qar,qbr->ab/dot_general | solution.py:23
  138.7 0.0 reduce-scatter.2.cloned.1.call-update
  138.7 18.3 %reduce-scatter.2.cloned.1.call-done = f32[64,128]{1,0:T(8,128)} async-done(((f32[64,512]{1,0:T(8,128)}), f32[64,128]{1,0:T(8,128)}) %reduce-scatter.2.cloned.1.call-update) | async-done | bytes 32784 | tf_op jit(solution)/shard_map/reduce_scatter | solution.py:29
  157.0 1.4 broadcast_multiply_fusion
Async XLA Ops:
  6.5 0.9 copy-start
  10.9 9.9 %copy-start.1 = (bf16[64,128]{1,0:T(8,128)(2,1)S(1)}, bf16[64,128]{1,0:T(8,128)(2,1)}, u32[]{:S(2)}) copy-start(bf16[64,128]{1,0:T(8,128)(2,1)} %param.4) | copy-start | bytes 49156
  16.5 19.9 %all-to-all-start = ((bf16[4,2,65536]{2,1,0:T(2,128)(2,1)}), bf16[4,2,65536]{2,1,0:T(2,128)(2,1)S(1)}, u32[]{:S(2)}, u32[]{:S(2)}) async-start(bf16[4,2,65536]{2,1,0:T(2,128)(2,1)} %reshape.10), calls=%async_computation | async-start | bytes 2097152 | tf_op jit(solution)/shard_map/all_to_all | solution.py:17
  20.8 113.7 %all-gather.2.cloned.1.call-start = ((), (), s32[]{:S(2)}) async-start(), calls=%async_computation.3 | async-start | bytes 4718592 | tf_op jit(solution)/shard_map/all_gather | solution.py:26
  60.5 96.5 %reduce-scatter.2.cloned.1.call-start = ((), (), s32[]{:S(2)}) async-start(), calls=%async_computation.4 | async-start | bytes 163840 | tf_op jit(solution)/shard_map/reduce_scatter | solution.py:29
Sparse Core Ops, SparseCore 0:
  60.6 73.7 all-gather.1
  138.8 18.1 reduce-scatter.1
where the time goes:
time: 166 us; the launch traced here: 165 us
  waiting for transfers between devices  92.3 us (56%)
  blocking collectives  26.8 us (16%)
  local copies, waits for them, and re-layouts  18.9 us (11%)
  between operations  13.5 us (8%)
  matrix products  8.09 us (5%)
  starting transfers between devices  4.3 us (3%)
    all_gather x1, waiting for transfers between devices, on_device(): lax.all_gather(rounded, 'row', axis=1, tiled=True)  73.9 us
    reduce_scatter x1, waiting for transfers between devices, on_device(): lax.psum_scatter(partial_gram, 'col', scatter_dimension=1, tiled=True)  18.3 us
    all_gather x1, blocking collectives, on_device(): whole_factor = lax.all_gather(basis_two, 'col', axis=0, tiled=True)  15.6 us
    all_to_all x1, blocking collectives, on_device(): lax.all_to_all(full.astype(jnp.bfloat16), 'col', split_axis=0, concat_axi...  11.2 us
    unnamed x8, local copies, waits for them, and re-layouts  6.55 us
    all_to_all x2, local copies, waits for them, and re-layouts, on_device(): lax.all_to_all(inner, 'col', split_axis=2, concat_axis=1, tiled=True)  6.45 us
    all_to_all x1, starting transfers between devices, on_device(): lax.all_to_all(inner, 'col', split_axis=2, concat_axis=1, tiled=True)  4.26 us
    dot_general x1, matrix products, on_device(): jnp.einsum('qar,qbr->ab', rounded, lax.all_gather(rounded, 'row', axis=1,...  4.22 us
  transfers between devices with their start and end apart: 3, of which 2 were waited for; matrix products, arithmetic and copies ran while one was open for 0% of the time, Pallas kernels for 0%

commit v1 on v0

--- a/solution.py
+++ b/solution.py
@@ -2,6 +2,31 @@
 import jax.numpy as jnp
 from jax import lax
 from jax.sharding import PartitionSpec as P
+
+
+def laid_out(blocks, dim):
+    lengths = list(blocks.shape[1:])
+    lengths[dim] *= blocks.shape[0]
+    return jnp.moveaxis(blocks, 0, dim).reshape(lengths)
+
+
+def on_each_block(x, axis, dim, apply, out_dim):
+    size, mine, rows = (lax.axis_size(axis), lax.axis_index(axis), x.shape[dim])
+    right = [(i, (i + 1) % size) for i in range(size)]
+    downward = [(i, (i - 1) % size) for i in range(size)]
+    half = size // 2
+    blocks = {}
+    from_left = from_right = x
+    for lap in range(half + 1):
+        next_left = lax.ppermute(from_left, axis, right) if lap < half else None
+        next_right = lax.ppermute(from_right, axis, downward) if lap < size - half - 1 else None
+        blocks[-lap] = apply(from_left, (mine - lap) % size * rows)
+        if 0 < lap < size - half:
+            blocks[lap] = apply(from_right, (mine + lap) % size * rows)
+        from_left, from_right = (next_left, next_right)
+    blocks = jnp.stack([blocks[k] for k in sorted(blocks)])
+    blocks = blocks[(jnp.arange(size) - mine + half) % size]
+    return laid_out(blocks, out_dim)
 
 
 def on_device(snapshot, basis_two, basis_three):
@@ -20,11 +45,14 @@
     rounded = lax.all_to_all(
         full.astype(jnp.bfloat16), "col", split_axis=0, concat_axis=2, tiled=True
     )
-    partial_gram = jnp.einsum(
-        "qar,qbr->ab",
+    partial_gram = on_each_block(
         rounded,
-        lax.all_gather(rounded, "row", axis=1, tiled=True),
-        preferred_element_type=jnp.float32,
+        "row",
+        1,
+        lambda shard, offset: jnp.einsum(
+            "qar,qbr->ab", rounded, shard, preferred_element_type=jnp.float32
+        ),
+        1,
     )
     summed_gram = lax.psum_scatter(partial_gram, "col", scatter_dimension=1, tiled=True)
     return summed_gram * (1.0 / (ranks_two * ranks_three))

time: 166 us -> 183 us (1.10)
  starting transfers between devices: 4.3 us -> 42.2 us
  waiting for transfers between devices: 92.3 us -> 66.9 us
  matrix products: 8.09 us -> 11.8 us
    all_gather x1 -> x0, waiting for transfers between devices: 73.9 us -> none  [on_device(): lax.all_gather(rounded, 'row', axis=1, tiled=True)]
    ppermute x0 -> x7, waiting for transfers between devices: none -> 48.1 us  [the longest x4 48.1 us: on_each_block(): next_left = lax.ppermute(from_left, axis, right) if lap < half else None]
    ppermute x0 -> x7, starting transfers between devices: none -> 38 us  [the longest x3 30.7 us: on_each_block(): lax.ppermute(from_right, axis, downward)]
    dot_general x1 -> x8, matrix products: 4.22 us -> 7.99 us  [on_device(): jnp.einsum('qar,qbr->ab', rounded, shard, preferred_element_type=jnp.floa...]
    unnamed x8 -> x12, local copies, waits for them, and re-layouts: 6.55 us -> 6.57 us
  transfers between devices with their start and end apart: 3 -> 9, of which waited for: 2 -> 5; matrix products, arithmetic and copies ran while one was open for 0% -> 4% of each run, Pallas kernels for 0% -> 0%
where the time goes in v1:
time: 183 us; the launch traced here: 182 us
  waiting for transfers between devices  66.9 us (37%)
  starting transfers between devices  42.2 us (23%)
  blocking collectives  26.8 us (15%)
  local copies, waits for them, and re-layouts  19.7 us (11%)
  between operations  13.6 us (7%)
  matrix products  11.8 us (6%)
    ppermute x4, waiting for transfers between devices, on_each_block(): next_left = lax.ppermute(from_left, axis, right) if lap < half else None  48.1 us
    ppermute x3, starting transfers between devices, on_each_block(): lax.ppermute(from_right, axis, downward)  30.7 us
    reduce_scatter x1, waiting for transfers between devices, on_device(): lax.psum_scatter(partial_gram, 'col', scatter_dimension=1, tiled=True)  18.9 us
    all_gather x1, blocking collectives, on_device(): whole_factor = lax.all_gather(basis_two, 'col', axis=0, tiled=True)  15.6 us
    all_to_all x1, blocking collectives, on_device(): lax.all_to_all(full.astype(jnp.bfloat16), 'col', split_axis=0, concat_axi...  11.2 us
    dot_general x8, matrix products, on_device(): jnp.einsum('qar,qbr->ab', rounded, shard, preferred_element_type=jnp.floa...  7.99 us
    ppermute x4, starting transfers between devices, on_each_block(): next_left = lax.ppermute(from_left, axis, right) if lap < half else None  7.31 us
    unnamed x12, local copies, waits for them, and re-layouts  6.57 us
  transfers between devices with their start and end apart: 9, of which 5 were waited for; matrix products, arithmetic and copies ran while one was open for 4% of the time, Pallas kernels for 0%

profile of v1, /device:TPU:0, one launch (start us, length us, event | category | flops | bytes accessed | tf_op | source)
XLA Modules:
  0.0 182.5 jit_solution(4565947094073385699)
XLA Ops:
  6.5 0.0 copy-start
  6.5 0.9 copy-done
  7.4 3.4 %convolution_convert_fusion = bf16[4096,128]{1,0:T(8,128)(2,1)S(1)} fusion(bf16[4096,512]{1,0:T(8,128)(2,1)} %bitcast.95, bf16[512,128]{1,0:T(8,128)(2,1)S(1)} %copy-done), kind=kOutput, calls=%fused_computation.1 | convolution fusion | flops 537395200 | bytes 5373952 | tf_op jit(solution)/shard_map/dot_general | solution.py:36
  10.9 0.0 copy-start.3
  10.9 3.0 %copy.37 = bf16[64,64,128]{1,0,2:T(8,128)(2,1)S(1)} copy(bf16[64,64,128]{2,1,0:T(8,128)(2,1)S(1)} %bitcast.96) | data formatting | bytes 2097152 | tf_op jit(solution)/shard_map/reshape | solution.py:41
  13.9 2.7 %reshape.81 = bf16[4,2,65536]{2,1,0:T(2,128)(2,1)} reshape(bf16[128,64,64]{2,1,0:T(8,128)(2,1)S(1)} %bitcast.93) | data formatting | bytes 2097152
  16.5 4.3 %all-to-all-start = ((bf16[4,2,65536]{2,1,0:T(2,128)(2,1)}), bf16[4,2,65536]{2,1,0:T(2,128)(2,1)S(1)}, u32[]{:S(2)}, u32[]{:S(2)}) async-start(bf16[4,2,65536]{2,1,0:T(2,128)(2,1)} %reshape.81), calls=%async_computation | async-start | bytes 2097152 | tf_op jit(solution)/shard_map/all_to_all | solution.py:42
  20.8 0.0 reduce-scatter.2.cloned.1.call-start
  20.8 0.0 copy-done.3
  20.8 15.6 %all_gather.3 = bf16[256,128]{1,0:T(8,128)(2,1)S(1)} all-gather(bf16[64,128]{1,0:T(8,128)(2,1)S(1)} %copy-done.3), channel_id=1, replica_groups=mesh['row'=8,'col'=4] {'col'}, dimensions={0}, use_global_device_ids=true | all-gather | bytes 81920 | tf_op jit(solution)/shard_map/all_gather | solution.py:43
  36.4 0.0 all-to-all-done
  36.4 1.4 reshape.82
  37.9 2.9 %copy.39 = bf16[64,4,64,32]{2,1,3,0:T(4,128)(2,1)} copy(bf16[64,4,64,32]{2,0,3,1:T(8,128)(2,1)S(1)} %bitcast.94) | data formatting | bytes 2097152 | tf_op jit(solution)/shard_map/all_to_all | solution.py:42
  40.8 3.5 %all_to_all.29 = bf16[64,256,32]{1,2,0:T(8,128)(2,1)S(1)} reshape(bf16[64,4,64,32]{2,1,3,0:T(4,128)(2,1)} %copy.39) | data formatting | bytes 2097152 | tf_op jit(solution)/shard_map/all_to_all | solution.py:42
  44.3 0.4 fusion
  44.7 1.7 copy.40
  46.4 0.9 reshape.83
  47.3 11.2 %all_to_all.36 = bf16[4,2,32768]{2,1,0:T(2,128)(2,1)S(1)} all-to-all(bf16[4,2,32768]{2,1,0:T(2,128)(2,1)S(1)} %reshape.83), channel_id=1, replica_groups=mesh['row'=8,'col'=4] {'col'}, dimensions={0} | all-to-all | bytes 1048576 | tf_op jit(solution)/shard_map/all_to_all | solution.py:45
  58.5 0.7 reshape.84
  59.2 0.1 copy.41
  59.4 0.4 copy.42
  59.8 0.0 copy-start.2
  59.8 2.2 %collective-permute-start = (bf16[32,64,128]{2,1,0:T(8,128)(2,1)S(1)}, bf16[32,64,128]{2,1,0:T(8,128)(2,1)S(1)}, u32[]{:S(2)}, u32[]{:S(2)}) collective-permute-start(bf16[32,64,128]{2,1,0:T(8,128)(2,1)S(1)} %copy.42), channel_id=1, source_target_pairs={{0,4},{4,8},{8,12},{12,16},{16,20},{20,24},{24,28},{28,0},{1,5},{5... | collective-permute-start | bytes 1572872 | tf_op jit(solution)/shard_map/ppermute | solution.py:21
  62.0 14.6 %collective-permute-done = bf16[32,64,128]{2,1,0:T(8,128)(2,1)S(1)} collective-permute-done((bf16[32,64,128]{2,1,0:T(8,128)(2,1)S(1)}, bf16[32,64,128]{2,1,0:T(8,128)(2,1)S(1)}, u32[]{:S(2)}, u32[]{:S(2)}) %collective-permute-start) | collective-permute-done | bytes 524320 | tf_op jit(solution)/shard_map/ppermute | solution.py:21
  76.6 0.0 copy-done.2
  76.6 0.0 collective-permute-start.1
  76.6 4.7 %collective-permute-start.4 = (bf16[32,64,128]{2,1,0:T(8,128)(2,1)}, bf16[32,64,128]{2,1,0:T(8,128)(2,1)S(1)}, u32[]{:S(2)}, u32[]{:S(2)}) collective-permute-start(bf16[32,64,128]{2,1,0:T(8,128)(2,1)} %copy-done.2), channel_id=1, source_target_pairs={{0,28},{4,0},{8,4},{12,8},{16,12},{20,16},{24,20},{28,24},{1,29},{... | collective-permute-start | bytes 1572872 | tf_op jit(solution)/shard_map/ppermute | solution.py:22
  81.3 17.0 %collective-permute-done.1 = bf16[32,64,128]{2,1,0:T(8,128)(2,1)S(1)} collective-permute-done((bf16[32,64,128]{2,1,0:T(8,128)(2,1)S(1)}, bf16[32,64,128]{2,1,0:T(8,128)(2,1)S(1)}, u32[]{:S(2)}, u32[]{:S(2)}) %collective-permute-start.1) | collective-permute-done | bytes 524320 | tf_op jit(solution)/shard_map/ppermute | solution.py:21
  98.4 0.0 copy-start.1
  98.4 2.5 %collective-permute-start.2 = (bf16[32,64,128]{2,1,0:T(8,128)(2,1)S(1)}, bf16[32,64,128]{2,1,0:T(8,128)(2,1)}, u32[]{:S(2)}, u32[]{:S(2)}) collective-permute-start(bf16[32,64,128]{2,1,0:T(8,128)(2,1)S(1)} %collective-permute-done.1), channel_id=1, source_target_pairs={{0,4},{4,8},{8,12},{12,16},{16,20},{20,24},{24,28},{28,0},{1,5},{5... | collective-permute-start | bytes 1572872 | tf_op jit(solution)/shard_map/ppermute | solution.py:21
  100.8 0.0 collective-permute-done.4
  100.9 0.0 copy-done.1
  100.9 12.4 %collective-permute-start.5 = (bf16[32,64,128]{2,1,0:T(8,128)(2,1)S(1)}, bf16[32,64,128]{2,1,0:T(8,128)(2,1)}, u32[]{:S(2)}, u32[]{:S(2)}) collective-permute-start(bf16[32,64,128]{2,1,0:T(8,128)(2,1)S(1)} %collective-permute-done.4), channel_id=1, source_target_pairs={{0,28},{4,0},{8,4},{12,8},{16,12},{20,16},{24,20},{28,24},{1,29},{... | collective-permute-start | bytes 1572872 | tf_op jit(solution)/shard_map/ppermute | solution.py:22
  113.2 8.8 %collective-permute-done.2 = bf16[32,64,128]{2,1,0:T(8,128)(2,1)} collective-permute-done((bf16[32,64,128]{2,1,0:T(8,128)(2,1)S(1)}, bf16[32,64,128]{2,1,0:T(8,128)(2,1)}, u32[]{:S(2)}, u32[]{:S(2)}) %collective-permute-start.2) | collective-permute-done | bytes 524320 | tf_op jit(solution)/shard_map/ppermute | solution.py:21
  122.0 2.6 %collective-permute-start.3 = (bf16[32,64,128]{2,1,0:T(8,128)(2,1)}, bf16[32,64,128]{2,1,0:T(8,128)(2,1)}, u32[]{:S(2)}, u32[]{:S(2)}) collective-permute-start(bf16[32,64,128]{2,1,0:T(8,128)(2,1)} %collective-permute-done.2), channel_id=1, source_target_pairs={{0,4},{4,8},{8,12},{12,16},{16,20},{20,24},{24,28},{28,0},{1,5},{5... | collective-permute-start | bytes 1572872 | tf_op jit(solution)/shard_map/ppermute | solution.py:21
  124.6 0.0 collective-permute-done.5
  124.7 13.6 %collective-permute-start.6 = (bf16[32,64,128]{2,1,0:T(8,128)(2,1)}, bf16[32,64,128]{2,1,0:T(8,128)(2,1)S(1)}, u32[]{:S(2)}, u32[]{:S(2)}) collective-permute-start(bf16[32,64,128]{2,1,0:T(8,128)(2,1)} %collective-permute-done.5), channel_id=1, source_target_pairs={{0,28},{4,0},{8,4},{12,8},{16,12},{20,16},{24,20},{28,24},{1,29},{... | collective-permute-start | bytes 1572872 | tf_op jit(solution)/shard_map/ppermute | solution.py:22
  138.2 7.6 %collective-permute-done.3 = bf16[32,64,128]{2,1,0:T(8,128)(2,1)} collective-permute-done((bf16[32,64,128]{2,1,0:T(8,128)(2,1)}, bf16[32,64,128]{2,1,0:T(8,128)(2,1)}, u32[]{:S(2)}, u32[]{:S(2)}) %collective-permute-start.3) | collective-permute-done | bytes 524320 | tf_op jit(solution)/shard_map/ppermute | solution.py:21
  145.8 1.5 fusion.7
  147.3 1.5 fusion.6
  148.8 1.5 fusion.5
  150.4 0.5 fusion.4
  150.9 0.4 fusion.8
  151.3 0.5 fusion.3
  151.8 1.5 fusion.2
  153.4 0.0 collective-permute-done.6
  153.4 0.5 fusion.1
  153.9 0.6 gather_fusion
  154.5 0.2 copy.51
  154.6 0.8 reshape.63
  155.4 0.0 reduce-scatter.2.cloned.1.call-update
  155.4 18.9 %reduce-scatter.2.cloned.1.call-done = f32[64,128]{1,0:T(8,128)} async-done(((f32[64,512]{1,0:T(8,128)}), f32[64,128]{1,0:T(8,128)}) %reduce-scatter.2.cloned.1.call-update) | async-done | bytes 32784 | tf_op jit(solution)/shard_map/reduce_scatter | solution.py:57
  174.3 1.4 broadcast_multiply_fusion
  (2 shorter events, 0.0 us)
Async XLA Ops:
  6.5 0.9 copy-start
  10.9 9.9 %copy-start.3 = (bf16[64,128]{1,0:T(8,128)(2,1)S(1)}, bf16[64,128]{1,0:T(8,128)(2,1)}, u32[]{:S(2)}) copy-start(bf16[64,128]{1,0:T(8,128)(2,1)} %param.4) | copy-start | bytes 49156
  16.5 19.9 %all-to-all-start = ((bf16[4,2,65536]{2,1,0:T(2,128)(2,1)}), bf16[4,2,65536]{2,1,0:T(2,128)(2,1)S(1)}, u32[]{:S(2)}, u32[]{:S(2)}) async-start(bf16[4,2,65536]{2,1,0:T(2,128)(2,1)} %reshape.81), calls=%async_computation | async-start | bytes 2097152 | tf_op jit(solution)/shard_map/all_to_all | solution.py:42
  20.8 153.4 %reduce-scatter.2.cloned.1.call-start = ((), (), s32[]{:S(2)}) async-start(), calls=%async_computation.3 | async-start | bytes 163840 | tf_op jit(solution)/shard_map/reduce_scatter | solution.py:57
  59.8 16.8 %copy-start.2 = (bf16[32,64,128]{2,1,0:T(8,128)(2,1)}, bf16[32,64,128]{2,1,0:T(8,128)(2,1)S(1)}, u32[]{:S(2)}) copy-start(bf16[32,64,128]{2,1,0:T(8,128)(2,1)S(1)} %copy.42) | copy-start | bytes 1572868
  59.8 16.8 %collective-permute-start = (bf16[32,64,128]{2,1,0:T(8,128)(2,1)S(1)}, bf16[32,64,128]{2,1,0:T(8,128)(2,1)S(1)}, u32[]{:S(2)}, u32[]{:S(2)}) collective-permute-start(bf16[32,64,128]{2,1,0:T(8,128)(2,1)S(1)} %copy.42), channel_id=1, source_target_pairs={{0,4},{4,8},{8,12},{12,16},{16,20},{20,24},{24,28},{28,0},{1,5},{5... | collective-permute-start | bytes 1572872 | tf_op jit(solution)/shard_map/ppermute | solution.py:21
  76.6 21.8 %collective-permute-start.1 = (bf16[32,64,128]{2,1,0:T(8,128)(2,1)S(1)}, bf16[32,64,128]{2,1,0:T(8,128)(2,1)S(1)}, u32[]{:S(2)}, u32[]{:S(2)}) collective-permute-start(bf16[32,64,128]{2,1,0:T(8,128)(2,1)S(1)} %collective-permute-done), channel_id=1, source_target_pairs={{0,4},{4,8},{8,12},{12,16},{16,20},{20,24},{24,28},{28,0},{1,5},{5... | collective-permute-start | bytes 1572872 | tf_op jit(solution)/shard_map/ppermute | solution.py:21
  76.6 24.2 %collective-permute-start.4 = (bf16[32,64,128]{2,1,0:T(8,128)(2,1)}, bf16[32,64,128]{2,1,0:T(8,128)(2,1)S(1)}, u32[]{:S(2)}, u32[]{:S(2)}) collective-permute-start(bf16[32,64,128]{2,1,0:T(8,128)(2,1)} %copy-done.2), channel_id=1, source_target_pairs={{0,28},{4,0},{8,4},{12,8},{16,12},{20,16},{24,20},{28,24},{1,29},{... | collective-permute-start | bytes 1572872 | tf_op jit(solution)/shard_map/ppermute | solution.py:22
  98.4 2.5 %copy-start.1 = (bf16[32,64,128]{2,1,0:T(8,128)(2,1)}, bf16[32,64,128]{2,1,0:T(8,128)(2,1)S(1)}, u32[]{:S(2)}) copy-start(bf16[32,64,128]{2,1,0:T(8,128)(2,1)S(1)} %collective-permute-done.1) | copy-start | bytes 1572868
  98.4 23.7 %collective-permute-start.2 = (bf16[32,64,128]{2,1,0:T(8,128)(2,1)S(1)}, bf16[32,64,128]{2,1,0:T(8,128)(2,1)}, u32[]{:S(2)}, u32[]{:S(2)}) collective-permute-start(bf16[32,64,128]{2,1,0:T(8,128)(2,1)S(1)} %collective-permute-done.1), channel_id=1, source_target_pairs={{0,4},{4,8},{8,12},{12,16},{16,20},{20,24},{24,28},{28,0},{1,5},{5... | collective-permute-start | bytes 1572872 | tf_op jit(solution)/shard_map/ppermute | solution.py:21
  100.9 23.8 %collective-permute-start.5 = (bf16[32,64,128]{2,1,0:T(8,128)(2,1)S(1)}, bf16[32,64,128]{2,1,0:T(8,128)(2,1)}, u32[]{:S(2)}, u32[]{:S(2)}) collective-permute-start(bf16[32,64,128]{2,1,0:T(8,128)(2,1)S(1)} %collective-permute-done.4), channel_id=1, source_target_pairs={{0,28},{4,0},{8,4},{12,8},{16,12},{20,16},{24,20},{28,24},{1,29},{... | collective-permute-start | bytes 1572872 | tf_op jit(solution)/shard_map/ppermute | solution.py:22
  122.0 23.8 %collective-permute-start.3 = (bf16[32,64,128]{2,1,0:T(8,128)(2,1)}, bf16[32,64,128]{2,1,0:T(8,128)(2,1)}, u32[]{:S(2)}, u32[]{:S(2)}) collective-permute-start(bf16[32,64,128]{2,1,0:T(8,128)(2,1)} %collective-permute-done.2), channel_id=1, source_target_pairs={{0,4},{4,8},{8,12},{12,16},{16,20},{20,24},{24,28},{28,0},{1,5},{5... | collective-permute-start | bytes 1572872 | tf_op jit(solution)/shard_map/ppermute | solution.py:21
  124.7 28.7 %collective-permute-start.6 = (bf16[32,64,128]{2,1,0:T(8,128)(2,1)}, bf16[32,64,128]{2,1,0:T(8,128)(2,1)S(1)}, u32[]{:S(2)}, u32[]{:S(2)}) collective-permute-start(bf16[32,64,128]{2,1,0:T(8,128)(2,1)} %collective-permute-done.5), channel_id=1, source_target_pairs={{0,28},{4,0},{8,4},{12,8},{16,12},{20,16},{24,20},{28,24},{1,29},{... | collective-permute-start | bytes 1572872 | tf_op jit(solution)/shard_map/ppermute | solution.py:22
Sparse Core Ops, SparseCore 0:
  155.5 18.6 reduce-scatter.1
